TPU v7x, 256 devices: a whole 4x4x8 slice. The times are simulated.
256 devices in a mesh: cfg: 2 (over y_hi), seq: 16 (over z, core), tp: 8 (over y_lo, x).
Axes of the slice: x: 4, y: 4 (y_hi: 2, y_lo: 2; y = y_hi * 2 + y_lo), z: 8, core: 2. Of those that a mesh axis runs over, the one named last changes fastest.
Arguments:
- queries: bfloat16 [2, 7680, 5120], P('cfg', 'seq', 'tp'), may hold values from -5 to 5
- keys: bfloat16 [2, 7680, 5120], P('cfg', 'seq', 'tp'), may hold values from -5 to 5
- values: bfloat16 [2, 7680, 5120], P('cfg', 'seq', 'tp'), may hold values from -5 to 5
- text_keys: bfloat16 [2, 512, 5120], P('cfg', None, 'tp'), may hold values from -7.5 to 7.5
- text_values: bfloat16 [2, 512, 5120], P('cfg', None, 'tp'), may hold values from -5 to 5
- prompt_lengths: int32 [2], P('cfg'), may hold values from 64 to 512
- frame_counts: int32 [16], P('seq'), may hold values from 240 to 480
- out_weight: bfloat16 [5120, 5120], P('tp'), may hold values from -0.5 to 0.5
Outputs:
- velocity: bfloat16 [7680, 5120], P('seq', ('tp', 'cfg'))
All inputs are finite; a program needn't handle non-finite values.
Results may differ from a plain program's by a relative error of at most 0.015.
Values may be sent and summed in bfloat16 or wider, within the bound.
A program may use at most 256 MiB of HBM per device.

v0:
```python
import jax
import jax.numpy as jnp
from jax import lax
from jax.sharding import PartitionSpec as P

HEAD_DIM = 128
FRAME_SLOTS = 480
GUIDANCE = 5.0
RESCALE = 0.7
NEGATIVE = -1e30


def in_order(pieces, dim):
    dims = list(pieces.shape[1:])
    dims[dim] *= pieces.shape[0]
    return jnp.moveaxis(pieces, 0, dim).reshape(dims)


def from_everyone(value, axis):
    devices = lax.axis_size(axis)
    return lax.all_to_all(
        jnp.broadcast_to(value[None], (devices, *value.shape)), axis, 0, 0, tiled=True
    )


def gathered_copies(value, axis, dim):
    return in_order(from_everyone(value, axis), dim)


def of_everyone(value, axis):
    return from_everyone(value, axis).sum(axis=0)


def together(arrays, axis):
    ends = [0]
    for a in arrays:
        ends.append(ends[-1] + a.size)
    running = of_everyone(jnp.concatenate([a.ravel() for a in arrays]), axis)
    return tuple((running[b:e].reshape(a.shape) for a, b, e in zip(arrays, ends, ends[1:])))


def frame_valid(positions, counts_table):
    frame_index = positions // FRAME_SLOTS
    slot_index = positions % FRAME_SLOTS
    frame_ids = jnp.arange(counts_table.shape[0], dtype=jnp.int32)
    frame_limit = jnp.sum(
        jnp.where(frame_index[:, None] == frame_ids[None, :], counts_table[None, :], 0), axis=1
    )
    return slot_index < frame_limit


def attend_block(carry, key_rows, value_rows, query_heads, key_mask):
    row_max, weight_sum, mixed_sum = carry
    head_count = query_heads.shape[1]
    key_heads = key_rows.reshape(key_rows.shape[0], head_count, HEAD_DIM)
    value_heads = value_rows.reshape(value_rows.shape[0], head_count, HEAD_DIM)
    scores = jnp.einsum(
        "qhd,khd->hqk", query_heads, key_heads, preferred_element_type=jnp.float32
    ) * HEAD_DIM ** (-0.5)
    scores = jnp.where(key_mask[None, None, :], scores, NEGATIVE)
    new_max = jnp.maximum(row_max, jnp.max(scores, axis=2))
    shrink = jnp.exp(row_max - new_max)
    weights = jnp.exp(scores - new_max[:, :, None])
    weight_sum = weight_sum * shrink + jnp.sum(weights, axis=2)
    mixed_sum = mixed_sum * shrink[:, :, None] + jnp.einsum(
        "hqk,khd->hqd",
        weights.astype(jnp.bfloat16),
        value_heads,
        preferred_element_type=jnp.float32,
    )
    return (new_max, weight_sum, mixed_sum)


def body(queries, keys, values, text_keys, text_values, prompt_lengths, frame_counts, out_weight):
    row_count = queries.shape[1]
    head_cols = queries.shape[2]
    head_count = head_cols // HEAD_DIM
    all_counts = gathered_copies(frame_counts, "seq", 0)
    query_heads = queries[0].reshape(row_count, head_count, HEAD_DIM)
    text_mask = jnp.arange(text_keys.shape[1], dtype=jnp.int32) < prompt_lengths[0]
    empty_state = (
        jnp.full((head_count, row_count), NEGATIVE, jnp.float32),
        jnp.zeros((head_count, row_count), jnp.float32),
        jnp.zeros((head_count, row_count, HEAD_DIM), jnp.float32),
    )
    text_state = attend_block(empty_state, text_keys[0], text_values[0], query_heads, text_mask)
    key_rows = lax.all_gather(keys[0], "seq", axis=0, tiled=True)
    value_rows = lax.all_gather(values[0], "seq", axis=0, tiled=True)
    positions = jnp.arange(key_rows.shape[0], dtype=jnp.int32)
    row_max, weight_sum, mixed_sum = attend_block(
        text_state, key_rows, value_rows, query_heads, frame_valid(positions, all_counts)
    )
    attended = (
        jnp.transpose(mixed_sum / weight_sum[:, :, None], (1, 0, 2))
        .reshape(row_count, head_cols)
        .astype(jnp.bfloat16)
    )
    projected = (
        lax.psum_scatter(
            lax.dot_general(
                out_weight, attended, (((0,), (1,)), ((), ())), preferred_element_type=jnp.float32
            ).astype(jnp.bfloat16),
            "tp",
            scatter_dimension=0,
            tiled=True,
        )
        .astype(jnp.float32)
        .T
    )
    branch = projected.astype(jnp.bfloat16)[None]
    paired = lax.all_to_all(branch, "cfg", split_axis=2, concat_axis=0, tiled=True)
    conditional = paired[0].astype(jnp.float32)
    unconditional = paired[1].astype(jnp.float32)
    guided = unconditional + GUIDANCE * (conditional - unconditional)
    token_weights = frame_valid(jnp.arange(row_count, dtype=jnp.int32), frame_counts).astype(
        jnp.float32
    )

    def local_sum(field_rows):
        return jnp.dot(token_weights, field_rows)

    guided_sum, guided_square, cond_sum, cond_square = together(
        (
            local_sum(guided),
            local_sum(guided * guided),
            local_sum(conditional),
            local_sum(conditional * conditional),
        ),
        "seq",
    )
    valid_total = jnp.sum(all_counts).astype(jnp.float32)
    guided_mean = guided_sum / valid_total
    guided_var = guided_square / valid_total - guided_mean * guided_mean
    cond_mean = cond_sum / valid_total
    cond_var = cond_square / valid_total - cond_mean * cond_mean
    std_ratio = jnp.sqrt((cond_var + 1.0) / (guided_var + 1.0))
    factor = RESCALE * std_ratio + (1.0 - RESCALE)
    return (guided_mean + (guided - guided_mean) * factor).astype(jnp.bfloat16)


def solution(mesh):
    placed = (
        P("cfg", "seq", "tp"),
        P("cfg", "seq", "tp"),
        P("cfg", "seq", "tp"),
        P("cfg", None, "tp"),
        P("cfg", None, "tp"),
        P("cfg"),
        P("seq"),
        P("tp", None),
    )
    return jax.shard_map(
        body, mesh=mesh, in_specs=placed, out_specs=P("seq", ("tp", "cfg")), check_vma=False
    )
```

profile of v0, /device:TPU:1, one launch (start us, length us, event | category | flops | bytes accessed | tf_op | source)
XLA Modules:
  0.0 327.0 jit_solution(5678599585954011462)
XLA Ops:
  9.3 10.0 %all-to-all-start = ((s32[16,1,1]{2,1,0:T(1,128)}), s32[16,1,1]{2,1,0:T(1,128)S(1)}, u32[]{:S(2)}, u32[]{:S(2)}) async-start(s32[16,1,1]{2,1,0:T(1,128)} %broadcast_in_dim.95), calls=%async_computation | async-start | bytes 16384 | tf_op jit(solution)/shard_map/all_to_all | solution.py:21
  19.3 1.3 copy.70
  21.2 1.3 copy.71
  22.6 3.2 fusion.7
  27.4 48.6 %all-gather.5.cloned.1.call-done = bf16[1,7680,640]{2,1,0:T(8,128)(2,1)} async-done(((bf16[1,480,640]{2,1,0:T(8,128)(2,1)}), bf16[1,7680,640]{2,1,0:T(8,128)(2,1)}) %all-gather.5.cloned.1.call-update) | async-done | bytes 9830416 | tf_op jit(solution)/shard_map/all_gather | solution.py:87
  76.0 13.7 %copy.76 = bf16[1,7680,640]{1,2,0:T(8,128)(2,1)} copy(bf16[1,7680,640]{2,1,0:T(8,128)(2,1)} %all-gather.5.cloned.1.call-done) | data formatting | bytes 19660800 | tf_op jit(solution)/shard_map/all_gather | solution.py:87
  89.8 31.7 %fusion = (f32[5,480]{1,0:T(8,128)S(1)}, f32[5,480,7680]{2,1,0:T(8,128)}) fusion(pred[7680]{0:T(1024)(128)(4,1)S(1)} %fusion.41, bf16[480,5,128]{0,2,1:T(8,128)(2,1)S(1)} %bitcast.102, bf16[7680,5,128]{0,2,1:T(8,128)(2,1)} %bitcast.97), kind=kOutput, calls=%fused_computation.2 | convolution fusion | flops 4773885440 | bytes 84190080 | tf_op jit(solution)/shard_map/qhd,khd->hqk/dot_general | solution.py:57
  121.5 3.9 %fusion.8 = f32[5,480]{1,0:T(8,128)S(1)} fusion(f32[5,480,512]{2,1,0:T(8,128)} %get-tuple-element.17, f32[5,480]{1,0:T(8,128)S(1)} %get-tuple-element.11, pred[512]{0:T(512)(128)(4,1)S(1)} %iota_compare_fusion.2), kind=kLoop, calls=%fused_computation.12 | loop fusion | flops 4912800 | bytes 4934912 | tf_op jit(solution)/shard_map/reduce_sum | solution.py:64
  125.4 23.8 %fusion.1 = f32[5,480]{1,0:T(8,128)S(1)} fusion(f32[5,480,7680]{2,1,0:T(8,128)} %get-tuple-element.15, f32[5,480]{1,0:T(8,128)S(1)} %get-tuple-element.10, pred[7680]{0:T(1024)(128)(4,1)S(1)} %fusion.41), kind=kLoop, calls=%fused_computation.3 | loop fusion | flops 73725600 | bytes 73754880 | tf_op jit(solution)/shard_map/reduce_sum | solution.py:64
  149.3 1.7 fusion.28
  151.0 13.7 %copy.79 = bf16[1,7680,640]{1,2,0:T(8,128)(2,1)} copy(bf16[1,7680,640]{2,1,0:T(8,128)(2,1)} %all-gather.7.cloned.1.call-done) | data formatting | bytes 19660800 | tf_op jit(solution)/shard_map/all_gather | solution.py:88
  164.7 29.4 %fusion.34 = bf16[480,5,128]{2,0,1:T(8,128)(2,1)S(1)} fusion(f32[480,5,128]{2,0,1:T(8,128)S(1)} %fusion.28, bf16[7680,5,128]{0,2,1:T(8,128)(2,1)} %bitcast.100, f32[5,480,7680]{2,1,0:T(8,128)} %get-tuple-element.15, f32[5,480]{1,0:T(8,128)S(1)} %get-tuple-element.10, pred[7680]{0:T(1024)(128)(4,1)S(1)} %fusion.41, f32[480,5]{0,1:T(8,128)S(1)} %get-tuple-element.7), kind=kOutput, calls=%fused_computation.25 | convolution fusion | flops 4793241600 | bytes 85428480 | tf_op jit(solution)/shard_map/hqk,khd->hqd/dot_general | solution.py:65
  194.3 8.8 %fusion.6 = bf16[5120,480]{0,1:T(8,128)(2,1)} fusion(bf16[480,640]{0,1:T(8,128)(2,1)S(1)} %bitcast.116, bf16[640,5120]{1,0:T(8,128)(2,1)} %param.15), kind=kOutput, calls=%fused_computation.8 | convolution fusion | flops 3148185600 | bytes 12083200 | tf_op jit(solution)/shard_map/dot_general | solution.py:100
  203.2 7.8 %copy.91 = bf16[5120,480]{1,0:T(8,128)(2,1)} copy(bf16[5120,480]{0,1:T(8,128)(2,1)} %fusion.6) | data formatting | bytes 9830400
  211.0 64.1 %reduce-scatter.4.cloned.1.call-done = bf16[640,480]{1,0:T(8,128)(2,1)} async-done(((bf16[5120,480]{1,0:T(8,128)(2,1)}), bf16[640,480]{1,0:T(8,128)(2,1)}) %reduce-scatter.4.cloned.1.call-update) | async-done | bytes 614416
  275.1 1.4 copy.92
  276.5 1.9 copy.82
  278.9 4.8 %reduce.13 = bf16[640,480]{1,0:T(8,128)(2,1)S(1)} reduce(bf16[640,1,480]{2,1,0:T(2,128)(2,1)S(1)} %bitcast.103, bf16[]{:T(256)} %broadcast.122), dimensions={1}, to_apply=%bitcast.78.reduce_sub_computation | reduce | bytes 1228802
  283.7 2.2 reshape.116
  285.9 3.7 %all-to-all-start.1 = ((bf16[2,2,76800]{2,1,0:T(2,128)(2,1)}), bf16[2,2,76800]{2,1,0:T(2,128)(2,1)S(1)}, u32[]{:S(2)}, u32[]{:S(2)}) async-start(bf16[2,2,76800]{2,1,0:T(2,128)(2,1)} %reshape.116), calls=%async_computation.1 | async-start | bytes 1228800 | tf_op jit(solution)/shard_map/all_to_all | solution.py:111
  289.7 9.5 %all-to-all-done.1 = bf16[2,2,76800]{2,1,0:T(2,128)(2,1)S(1)} async-done(((bf16[2,2,76800]{2,1,0:T(2,128)(2,1)}), bf16[2,2,76800]{2,1,0:T(2,128)(2,1)S(1)}, u32[]{:S(2)}, u32[]{:S(2)}) %all-to-all-start.1) | async-done | bytes 614432 | tf_op jit(solution)/shard_map/all_to_all | solution.py:111
  299.2 1.3 reshape.117
  302.4 8.9 %all-to-all-start.2 = ((f32[16,1,1280]{2,1,0:T(1,128)}), f32[16,1,1280]{2,1,0:T(1,128)S(1)}, u32[]{:S(2)}, u32[]{:S(2)}) async-start(f32[16,1,1280]{2,1,0:T(1,128)} %broadcast_in_dim.102), calls=%async_computation.2 | async-start | bytes 163840 | tf_op jit(solution)/shard_map/all_to_all | solution.py:21
  311.9 7.5 %all-to-all-done.2 = f32[16,1,1280]{2,1,0:T(1,128)S(1)} async-done(((f32[16,1,1280]{2,1,0:T(1,128)}), f32[16,1,1280]{2,1,0:T(1,128)S(1)}, u32[]{:S(2)}, u32[]{:S(2)}) %all-to-all-start.2) | async-done | bytes 81952 | tf_op jit(solution)/shard_map/all_to_all | solution.py:21
  (38 shorter events, 7.4 us)
Async XLA Ops:
  6.5 19.3 %copy-start = (bf16[1,512,640]{2,1,0:T(8,128)(2,1)S(1)}, bf16[1,512,640]{2,1,0:T(8,128)(2,1)}, u32[]{:S(2)}) copy-start(bf16[1,512,640]{2,1,0:T(8,128)(2,1)} %param.12) | copy-start | bytes 1966084
  6.5 69.5 %all-gather.5.cloned.1.call-start = ((), (), s32[]{:S(2)}) async-start(), calls=%async_computation.4 | async-start | bytes 10444800 | tf_op jit(solution)/shard_map/all_gather | solution.py:87
  7.3 143.7 %all-gather.7.cloned.1.call-start = ((), (), s32[]{:S(2)}) async-start(), calls=%async_computation.5 | async-start | bytes 10444800 | tf_op jit(solution)/shard_map/all_gather | solution.py:88
  9.3 16.9 %all-to-all-start = ((s32[16,1,1]{2,1,0:T(1,128)}), s32[16,1,1]{2,1,0:T(1,128)S(1)}, u32[]{:S(2)}, u32[]{:S(2)}) async-start(s32[16,1,1]{2,1,0:T(1,128)} %broadcast_in_dim.95), calls=%async_computation | async-start | bytes 16384 | tf_op jit(solution)/shard_map/all_to_all | solution.py:21
  19.2 255.8 %reduce-scatter.4.cloned.1.call-start = ((), (), s32[]{:S(2)}) async-start(), calls=%async_computation.6 | async-start | bytes 5898240
  121.5 27.8 %slice-start = ((s8[4915200]{0:T(1024)(128)(4,1)}), s8[4194304]{0:T(1024)(128)(4,1)S(1)}, s32[]{:S(2)}) async-start(s8[4915200]{0:T(1024)(128)(4,1)} %bitcast.98), calls=%async_computation.7 | async-start | bytes 8388608
  125.4 23.9 %slice-start.1 = ((s8[4915200]{0:T(1024)(128)(4,1)}), s8[720896]{0:T(1024)(128)(4,1)S(1)}, s32[]{:S(2)}) async-start(s8[4915200]{0:T(1024)(128)(4,1)} %bitcast.98), calls=%async_computation.8 | async-start | bytes 1441792
  285.9 13.3 %all-to-all-start.1 = ((bf16[2,2,76800]{2,1,0:T(2,128)(2,1)}), bf16[2,2,76800]{2,1,0:T(2,128)(2,1)S(1)}, u32[]{:S(2)}, u32[]{:S(2)}) async-start(bf16[2,2,76800]{2,1,0:T(2,128)(2,1)} %reshape.116), calls=%async_computation.1 | async-start | bytes 1228800 | tf_op jit(solution)/shard_map/all_to_all | solution.py:111
  302.4 17.0 %all-to-all-start.2 = ((f32[16,1,1280]{2,1,0:T(1,128)}), f32[16,1,1280]{2,1,0:T(1,128)S(1)}, u32[]{:S(2)}, u32[]{:S(2)}) async-start(f32[16,1,1280]{2,1,0:T(1,128)} %broadcast_in_dim.102), calls=%async_computation.2 | async-start | bytes 163840 | tf_op jit(solution)/shard_map/all_to_all | solution.py:21
Sparse Core Ops, SparseCore 0:
  9.2 66.8 all-gather.4
  77.9 61.1 all-gather.6
  211.1 63.8 reduce-scatter.3
where the time goes:
time: 328 us; the launch traced here: 327 us
  waiting for transfers between devices  131 us (40%)
  matrix products  75.7 us (23%)
  local copies, waits for them, and re-layouts  47.3 us (14%)
  other arithmetic  34.9 us (11%)
  starting transfers between devices  22.6 us (7%)
  between operations  15.2 us (5%)
    unnamed x4, waiting for transfers between devices  65.5 us
    all_gather x1, waiting for transfers between devices, body(): key_rows = lax.all_gather(keys[0], 'seq', axis=0, tiled=True)  48.6 us
    dot_general x2, matrix products, attend_block(): jnp.einsum('qhd,khd->hqk', query_heads, key_heads, preferred_element_type...  34.9 us
    dot_general x2, matrix products, attend_block(): jnp.einsum('hqk,khd->hqd', weights.astype(jnp.bfloat16), value_heads, pre...  31 us
    reduce_sum x2, other arithmetic, attend_block(): weight_sum = weight_sum * shrink + jnp.sum(weights, axis=2)  27.8 us
    all_to_all x2, starting transfers between devices, from_everyone(): lax.all_to_all(jnp.broadcast_to(value[None], (devices, *value.shape)), ax...  18.8 us
    unnamed x15, local copies, waits for them, and re-layouts  16.3 us
    all_gather x1, local copies, waits for them, and re-layouts, body(): value_rows = lax.all_gather(values[0], 'seq', axis=0, tiled=True)  13.7 us
  transfers between devices with their start and end apart: 6, of which 5 were waited for; matrix products, arithmetic and copies ran while one was open for 25% of the time, Pallas kernels for 0%

commit v1 on v0

--- a/solution.py
+++ b/solution.py
@@ -84,7 +84,9 @@
         jnp.zeros((head_count, row_count, HEAD_DIM), jnp.float32),
     )
     text_state = attend_block(empty_state, text_keys[0], text_values[0], query_heads, text_mask)
-    key_rows = lax.all_gather(keys[0], "seq", axis=0, tiled=True)
+    key_rows = jnp.concatenate(
+        lax.all_to_all(jnp.stack([keys[0]] * lax.axis_size("seq")), "seq", 0, 0), axis=0
+    )
     value_rows = lax.all_gather(values[0], "seq", axis=0, tiled=True)
     positions = jnp.arange(key_rows.shape[0], dtype=jnp.int32)
     row_max, weight_sum, mixed_sum = attend_block(

time: 328 us -> 557 us (1.70)
  waiting for transfers between devices: 131 us -> 337 us
  blocking collectives: 0 us -> 16.8 us
  local copies, waits for them, and re-layouts: 47.3 us -> 58.5 us
    all_to_all x0 -> x1, waiting for transfers between devices: none -> 254 us  [body(): lax.all_to_all(jnp.stack([keys[0]] * lax.axis_size('seq')), 'seq', 0, 0)]
    all_gather x1 -> x0, waiting for transfers between devices: 48.6 us -> none  [body(): key_rows = lax.all_gather(keys[0], 'seq', axis=0, tiled=True)]
    another operation x0 -> x2, local copies, waits for them, and re-layouts: none -> 27.6 us  [the longest x1 22 us: attend_block(): key_heads = key_rows.reshape(key_rows.shape[0], head_count, HEAD_DIM)]
    all_to_all x0 -> x1, blocking collectives: none -> 16.8 us  [from_everyone(): lax.all_to_all(jnp.broadcast_to(value[None], (devices, *value.shape)), ax...]
    all_gather x1 -> x0, local copies, waits for them, and re-layouts: 13.7 us -> none  [body(): key_rows = lax.all_gather(keys[0], 'seq', axis=0, tiled=True)]
    all_to_all x2 -> x1, starting transfers between devices: 18.8 us -> 8.92 us  [from_everyone(): lax.all_to_all(jnp.broadcast_to(value[None], (devices, *value.shape)), ax...]
    unnamed x15 -> x19, local copies, waits for them, and re-layouts: 16.3 us -> 14.2 us
    unnamed x4 -> x3, waiting for transfers between devices: 65.5 us -> 65.7 us
  transfers between devices with their start and end apart: 6 -> 5, of which waited for: 5 -> 4; matrix products, arithmetic and copies ran while one was open for 25% -> 16% of each run, Pallas kernels for 0% -> 0%
where the time goes in v1:
time: 557 us; the launch traced here: 556 us
  waiting for transfers between devices  337 us (61%)
  matrix products  76.1 us (14%)
  local copies, waits for them, and re-layouts  58.5 us (11%)
  other arithmetic  34.2 us (6%)
  starting transfers between devices  18 us (3%)
  blocking collectives  16.8 us (3%)
  between operations  15.5 us (3%)
    all_to_all x1, waiting for transfers between devices, body(): lax.all_to_all(jnp.stack([keys[0]] * lax.axis_size('seq')), 'seq', 0, 0)  254 us
    unnamed x3, waiting for transfers between devices  65.7 us
    dot_general x2, matrix products, attend_block(): jnp.einsum('qhd,khd->hqk', query_heads, key_heads, preferred_element_type...  35.4 us
    dot_general x2, matrix products, attend_block(): jnp.einsum('hqk,khd->hqd', weights.astype(jnp.bfloat16), value_heads, pre...  31 us
    reduce_sum x2, other arithmetic, attend_block(): weight_sum = weight_sum * shrink + jnp.sum(weights, axis=2)  27 us
    another operation x1, local copies, waits for them, and re-layouts, attend_block(): key_heads = key_rows.reshape(key_rows.shape[0], head_count, HEAD_DIM)  22 us
    all_to_all x1, blocking collectives, from_everyone(): lax.all_to_all(jnp.broadcast_to(value[None], (devices, *value.shape)), ax...  16.8 us
    unnamed x19, local copies, waits for them, and re-layouts  14.2 us
  transfers between devices with their start and end apart: 5, of which 4 were waited for; matrix products, arithmetic and copies ran while one was open for 16% of the time, Pallas kernels for 0%

profile of v1, /device:TPU:1, one launch (start us, length us, event | category | flops | bytes accessed | tf_op | source)
XLA Modules:
  0.0 555.7 jit_solution(11802831380905195080)
XLA Ops:
  7.2 16.8 %all_to_all.32 = s32[16,1,1]{2,1,0:T(1,128)S(1)} all-to-all(s32[16,1,1]{2,1,0:T(1,128)S(1)} %broadcast_in_dim.95), channel_id=1, replica_groups=mesh['cfg'=2,'seq'=16,'tp'=8] {'seq'}, dimensions={0} | all-to-all | bytes 128 | tf_op jit(solution)/shard_map/all_to_all | solution.py:21
  24.0 5.6 %stack.3 = bf16[16,480,640]{2,1,0:T(8,128)(2,1)} broadcast(bf16[480,640]{1,0:T(8,128)(2,1)} %bitcast.115), dimensions={1,2} | broadcast | bytes 10444800 | tf_op jit(solution)/shard_map/stack | solution.py:88
  29.6 5.3 all-to-all-start.1
  37.2 3.1 fusion.9
  41.5 253.9 %all-to-all-done.1 = bf16[16,480,640]{2,1,0:T(8,128)(2,1)} async-done(((bf16[16,480,640]{2,1,0:T(8,128)(2,1)}), bf16[16,480,640]{2,1,0:T(8,128)(2,1)}, u32[]{:S(2)}, u32[]{:S(2)}) %all-to-all-start.1) | async-done | bytes 9830432 | tf_op jit(solution)/shard_map/all_to_all | solution.py:88
  295.3 22.0 %reshape.104 = bf16[7680,5,128]{2,1,0:T(8,128)(2,1)} reshape(bf16[16,480,640]{2,1,0:T(8,128)(2,1)} %all-to-all-done.1) | data formatting | bytes 19660800 | tf_op jit(solution)/shard_map/reshape;reshape | solution.py:55
  317.3 32.2 %fusion = (f32[5,480]{1,0:T(8,128)S(1)}, f32[5,480,7680]{2,1,0:T(8,128)}) fusion(pred[7680]{0:T(1024)(128)(4,1)S(1)} %fusion.43, bf16[480,5,128]{0,2,1:T(8,128)(2,1)S(1)} %bitcast.100, bf16[7680,5,128]{2,1,0:T(8,128)(2,1)} %reshape.104), kind=kOutput, calls=%fused_computation.2 | convolution fusion | flops 4773885440 | bytes 84190080 | tf_op jit(solution)/shard_map/qhd,khd->hqk/dot_general | solution.py:57
  349.6 3.8 fusion.10
  353.4 23.2 %fusion.1 = f32[5,480]{1,0:T(8,128)S(1)} fusion(f32[5,480,7680]{2,1,0:T(8,128)} %get-tuple-element.15, f32[5,480]{1,0:T(8,128)S(1)} %get-tuple-element.10, pred[7680]{0:T(1024)(128)(4,1)S(1)} %fusion.43), kind=kLoop, calls=%fused_computation.3 | loop fusion | flops 73725600 | bytes 73754880 | tf_op jit(solution)/shard_map/reduce_sum | solution.py:64
  376.7 1.7 fusion.30
  378.4 13.7 %copy.79 = bf16[1,7680,640]{1,2,0:T(8,128)(2,1)} copy(bf16[1,7680,640]{2,1,0:T(8,128)(2,1)} %all-gather.3.cloned.1.call-done) | data formatting | bytes 19660800 | tf_op jit(solution)/shard_map/all_gather | solution.py:90
  392.1 29.3 %fusion.36 = bf16[480,5,128]{2,0,1:T(8,128)(2,1)S(1)} fusion(f32[480,5,128]{2,0,1:T(8,128)S(1)} %fusion.30, bf16[7680,5,128]{0,2,1:T(8,128)(2,1)} %bitcast.98, f32[5,480,7680]{2,1,0:T(8,128)} %get-tuple-element.15, f32[5,480]{1,0:T(8,128)S(1)} %get-tuple-element.10, pred[7680]{0:T(1024)(128)(4,1)S(1)} %fusion.43, f32[480,5]{0,1:T(8,128)S(1)} %get-tuple-element.7), kind=kOutput, calls=%fused_computation.27 | convolution fusion | flops 4793241600 | bytes 85428480 | tf_op jit(solution)/shard_map/hqk,khd->hqd/dot_general | solution.py:65
  421.7 8.8 %fusion.8 = bf16[5120,480]{0,1:T(8,128)(2,1)} fusion(bf16[480,640]{0,1:T(8,128)(2,1)S(1)} %bitcast.114, bf16[640,5120]{1,0:T(8,128)(2,1)} %param.15), kind=kOutput, calls=%fused_computation.10 | convolution fusion | flops 3148185600 | bytes 12083200 | tf_op jit(solution)/shard_map/dot_general | solution.py:102
  430.5 7.8 %copy.94 = bf16[5120,480]{1,0:T(8,128)(2,1)} copy(bf16[5120,480]{0,1:T(8,128)(2,1)} %fusion.8) | data formatting | bytes 9830400
  438.4 65.0 %reduce-scatter.4.cloned.1.call-done = bf16[640,480]{1,0:T(8,128)(2,1)} async-done(((bf16[5120,480]{1,0:T(8,128)(2,1)}), bf16[640,480]{1,0:T(8,128)(2,1)}) %reduce-scatter.4.cloned.1.call-update) | async-done | bytes 614416
  503.4 1.4 copy.95
  504.8 1.9 copy.82
  507.3 4.9 reduce.13
  512.2 2.2 reshape.112
  514.4 3.7 all-to-all-start.2
  518.1 9.5 %all-to-all-done.2 = bf16[2,2,76800]{2,1,0:T(2,128)(2,1)S(1)} async-done(((bf16[2,2,76800]{2,1,0:T(2,128)(2,1)}), bf16[2,2,76800]{2,1,0:T(2,128)(2,1)S(1)}, u32[]{:S(2)}, u32[]{:S(2)}) %all-to-all-start.2) | async-done | bytes 614432 | tf_op jit(solution)/shard_map/all_to_all | solution.py:113
  527.6 1.3 reshape.113
  530.8 8.9 %all-to-all-start.3 = ((f32[16,1,1280]{2,1,0:T(1,128)}), f32[16,1,1280]{2,1,0:T(1,128)S(1)}, u32[]{:S(2)}, u32[]{:S(2)}) async-start(f32[16,1,1280]{2,1,0:T(1,128)} %broadcast_in_dim.102), calls=%async_computation.3 | async-start | bytes 163840 | tf_op jit(solution)/shard_map/all_to_all | solution.py:21
  540.3 7.5 %all-to-all-done.3 = f32[16,1,1280]{2,1,0:T(1,128)S(1)} async-done(((f32[16,1,1280]{2,1,0:T(1,128)}), f32[16,1,1280]{2,1,0:T(1,128)S(1)}, u32[]{:S(2)}, u32[]{:S(2)}) %all-to-all-start.3) | async-done | bytes 81952 | tf_op jit(solution)/shard_map/all_to_all | solution.py:21
  (41 shorter events, 6.6 us)
Async XLA Ops:
  29.6 6.1 %copy-start.2 = (bf16[1,480,640]{2,1,0:T(8,128)(2,1)S(1)}, bf16[1,480,640]{2,1,0:T(8,128)(2,1)}, u32[]{:S(2)}) copy-start(bf16[1,480,640]{2,1,0:T(8,128)(2,1)} %param.8) | copy-start | bytes 1843204
  29.6 7.0 %copy-start = (bf16[1,512,640]{2,1,0:T(8,128)(2,1)S(1)}, bf16[1,512,640]{2,1,0:T(8,128)(2,1)}, u32[]{:S(2)}) copy-start(bf16[1,512,640]{2,1,0:T(8,128)(2,1)} %param.11) | copy-start | bytes 1966084
  29.6 7.3 %copy-start.1 = (bf16[1,512,640]{2,1,0:T(8,128)(2,1)S(1)}, bf16[1,512,640]{2,1,0:T(8,128)(2,1)}, u32[]{:S(2)}) copy-start(bf16[1,512,640]{2,1,0:T(8,128)(2,1)} %param.12) | copy-start | bytes 1966084
  29.6 265.7 %all-to-all-start.1 = ((bf16[16,480,640]{2,1,0:T(8,128)(2,1)}), bf16[16,480,640]{2,1,0:T(8,128)(2,1)}, u32[]{:S(2)}, u32[]{:S(2)}) async-start(bf16[16,480,640]{2,1,0:T(8,128)(2,1)} %stack.3), calls=%async_computation.1 | async-start | bytes 19660800 | tf_op jit(solution)/shard_map/all_to_all | solution.py:88
  34.9 343.4 %all-gather.3.cloned.1.call-start = ((), (), s32[]{:S(2)}) async-start(), calls=%async_computation.5 | async-start | bytes 10444800 | tf_op jit(solution)/shard_map/all_gather | solution.py:90
  35.7 467.7 %reduce-scatter.4.cloned.1.call-start = ((), (), s32[]{:S(2)}) async-start(), calls=%async_computation.6 | async-start | bytes 5898240
  349.6 27.1 %slice-start = ((s8[4915200]{0:T(1024)(128)(4,1)}), s8[4194304]{0:T(1024)(128)(4,1)S(1)}, s32[]{:S(2)}) async-start(s8[4915200]{0:T(1024)(128)(4,1)} %bitcast.96), calls=%async_computation.7 | async-start | bytes 8388608
  353.4 23.3 %slice-start.1 = ((s8[4915200]{0:T(1024)(128)(4,1)}), s8[720896]{0:T(1024)(128)(4,1)S(1)}, s32[]{:S(2)}) async-start(s8[4915200]{0:T(1024)(128)(4,1)} %bitcast.96), calls=%async_computation.8 | async-start | bytes 1441792
  514.4 13.2 %all-to-all-start.2 = ((bf16[2,2,76800]{2,1,0:T(2,128)(2,1)}), bf16[2,2,76800]{2,1,0:T(2,128)(2,1)S(1)}, u32[]{:S(2)}, u32[]{:S(2)}) async-start(bf16[2,2,76800]{2,1,0:T(2,128)(2,1)} %reshape.112), calls=%async_computation.2 | async-start | bytes 1228800 | tf_op jit(solution)/shard_map/all_to_all | solution.py:113
  530.8 17.0 %all-to-all-start.3 = ((f32[16,1,1280]{2,1,0:T(1,128)}), f32[16,1,1280]{2,1,0:T(1,128)S(1)}, u32[]{:S(2)}, u32[]{:S(2)}) async-start(f32[16,1,1280]{2,1,0:T(1,128)} %broadcast_in_dim.102), calls=%async_computation.3 | async-start | bytes 163840 | tf_op jit(solution)/shard_map/all_to_all | solution.py:21
Sparse Core Ops, SparseCore 0:
  37.6 196.1 all-gather.2
  438.5 64.8 reduce-scatter.3
